TPU v7x, 256 devices: a whole 4x4x8 slice. The times are simulated.
256 devices in a mesh: img: 16 (over x, z_lo, core), tp: 16 (over y, z_hi).
Axes of the slice: x: 4, y: 4, z: 8 (z_hi: 4, z_lo: 2; z = z_hi * 2 + z_lo), core: 2. Of those that a mesh axis runs over, the one named last changes fastest.
Arguments:
- patch_tokens: bfloat16 [32768, 1024], P(('img', 'tp')), may hold values from -12 to 12
- norm_gain: float32 [1024], replicated, may hold values from 0.1 to 1.9
- norm_bias: float32 [1024], replicated, may hold values from -3 to 3
- up_weight: bfloat16 [1024, 8192], P('img', 'tp'), may hold values from -0.1875 to 0.1875
- up_bias: float32 [8192], P('tp'), may hold values from -3 to 3
- down_weight: bfloat16 [8192, 4096], P('tp', 'img'), may hold values from -0.125 to 0.125
- down_bias: float32 [4096], replicated, may hold values from -3 to 3
Outputs:
- projected: bfloat16 [32768, 4096], P(('img', 'tp'))
All inputs are finite; a program needn't handle non-finite values.
Results may differ from a plain program's by a relative error of at most 0.014.
Values may be sent and summed in bfloat16 or wider, within the bound.
No kernel may reach another device: no remote copies, remote signals or barrier semaphores. Data moves between devices by JAX's collectives and lax.ppermute only.
A program may use at most 128 MiB of HBM per device.

v0:
```python
import jax
import jax.numpy as jnp
from jax import lax
from jax.sharding import PartitionSpec as P


def laid_out(parts, dim):
    dims = list(parts.shape[1:])
    dims[dim] *= parts.shape[0]
    return jnp.moveaxis(parts, 0, dim).reshape(dims)


def from_everyone(x, axis):
    copies = jnp.broadcast_to(x, (lax.axis_size(axis), *x.shape))
    return lax.all_to_all(copies, axis, split_axis=0, concat_axis=0, tiled=True)


def gather_directly(x, axis, dim):
    return laid_out(from_everyone(x, axis), dim)


def on_device(patch_tokens, norm_gain, norm_bias, up_weight, up_bias, down_weight, down_bias):
    values = lax.all_gather(patch_tokens, "tp", axis=0, tiled=True).astype(jnp.float32)
    center = jnp.mean(values, axis=1, keepdims=True)
    spread = jnp.mean((values - center) ** 2, axis=1, keepdims=True)
    gathered = ((values - center) * lax.rsqrt(spread + 1e-05) * norm_gain + norm_bias).astype(
        jnp.bfloat16
    )
    summed = jnp.dot(
        gathered, gather_directly(up_weight, "img", 0), preferred_element_type=jnp.float32
    )
    hidden = jax.nn.gelu(summed + up_bias).astype(jnp.bfloat16)
    down_full = lax.all_gather(down_weight, "img", axis=1, tiled=True)
    total = lax.psum_scatter(
        jnp.dot(hidden, down_full, preferred_element_type=jnp.float32).astype(jnp.bfloat16),
        "tp",
        scatter_dimension=0,
        tiled=True,
    ).astype(jnp.float32)
    return (total + down_bias).astype(jnp.bfloat16)


def solution(mesh):
    return jax.shard_map(
        on_device,
        mesh=mesh,
        in_specs=(P(("img", "tp"), None), P(), P(), P("img", "tp"), P("tp"), P("tp", "img"), P()),
        out_specs=P(("img", "tp"), None),
        check_vma=False,
    )
```

profile of v0, /device:TPU:1, one launch (start us, length us, event | category | flops | bytes accessed | tf_op | source)
XLA Modules:
  0.0 372.6 jit_solution(12355794440621910350)
XLA Ops:
  6.5 0.0 all-gather.3.cloned.1.call-start
  6.5 0.7 all-gather.3.cloned.1.call-update
  7.3 0.0 all-gather.5.cloned.1.call-start
  7.3 0.7 all-gather.5.cloned.1.call-update
  8.0 1.9 broadcast_in_dim.2
  9.9 7.2 %all-to-all-start = ((bf16[16,64,512]{2,1,0:T(8,128)(2,1)}), bf16[16,64,512]{2,1,0:T(8,128)(2,1)S(1)}, u32[]{:S(2)}, u32[]{:S(2)}) async-start(bf16[16,64,512]{2,1,0:T(8,128)(2,1)} %broadcast_in_dim.2), calls=%async_computation | async-start | bytes 2097152 | tf_op jit(solution)/shard_map/all_to_all | solution.py:15
  17.1 0.0 copy-start.2
  17.1 0.0 copy-start.3
  17.1 0.0 copy-start.4
  17.1 0.0 reduce-scatter.2.cloned.1.call-start
  17.2 72.1 %all-gather.3.cloned.1.call-done = bf16[2048,1024]{1,0:T(8,128)(2,1)} async-done(((bf16[128,1024]{1,0:T(8,128)(2,1)}), bf16[2048,1024]{1,0:T(8,128)(2,1)}) %all-gather.3.cloned.1.call-update) | async-done | bytes 4194320 | tf_op jit(solution)/shard_map/all_gather | solution.py:23
  89.2 0.0 copy-start
  89.2 3.0 convert_reduce_fusion
  92.2 0.5 copy-done
  92.7 1.4 fusion.2
  94.1 0.0 all-to-all-done
  94.1 47.1 %all-gather.5.cloned.1.call-done = bf16[512,4096]{1,0:T(8,128)(2,1)} async-done(((bf16[512,256]{1,0:T(8,128)(2,1)}), bf16[512,4096]{1,0:T(8,128)(2,1)}) %all-gather.5.cloned.1.call-update) | async-done | bytes 4194320 | tf_op jit(solution)/shard_map/all_gather | solution.py:33
  141.1 0.0 copy-done.2
  141.1 0.0 copy-done.3
  141.1 0.0 copy-done.4
  141.1 18.0 %convolution_convert_fusion = bf16[2048,4096]{1,0:T(8,128)(2,1)} fusion(bf16[512,4096]{1,0:T(8,128)(2,1)} %all-gather.5.cloned.1.call-done, bf16[1024,512]{1,0:T(8,128)(2,1)S(1)} %bitcast.3, bf16[2048,1024]{1,0:T(8,128)(2,1)} %all-gather.3.cloned.1.call-done, f32[1024]{0:T(1024)S(1)} %copy-done.2, f32[1024]{0:T(1024)S(1)} %copy-done.3, ...), kind=kOutput, calls=%fused_computation | convolution fusion | flops 10768875520 | bytes 26241024 | tf_op jit(solution)/shard_map/dot_general | solution.py:35
  159.1 0.0 copy-start.1
  159.1 0.0 reduce-scatter.2.cloned.1.call-update
  159.1 204.5 %reduce-scatter.2.cloned.1.call-done = bf16[128,4096]{1,0:T(8,128)(2,1)} async-done(((bf16[2048,4096]{1,0:T(8,128)(2,1)}), bf16[128,4096]{1,0:T(8,128)(2,1)}) %reduce-scatter.2.cloned.1.call-update) | async-done | bytes 1048592 | tf_op jit(solution)/shard_map/reduce_scatter | solution.py:34
  363.7 0.0 copy-done.1
  363.7 2.4 add_convert_fusion
  (2 shorter events, 0.0 us)
Async XLA Ops:
  6.5 82.7 %all-gather.3.cloned.1.call-start = ((), (), s32[]{:S(2)}) async-start(), calls=%async_computation.2 | async-start | bytes 4456448 | tf_op jit(solution)/shard_map/all_gather | solution.py:23
  7.3 133.9 %all-gather.5.cloned.1.call-start = ((), (), s32[]{:S(2)}) async-start(), calls=%async_computation.3 | async-start | bytes 4456448 | tf_op jit(solution)/shard_map/all_gather | solution.py:33
  9.9 84.1 %all-to-all-start = ((bf16[16,64,512]{2,1,0:T(8,128)(2,1)}), bf16[16,64,512]{2,1,0:T(8,128)(2,1)S(1)}, u32[]{:S(2)}, u32[]{:S(2)}) async-start(bf16[16,64,512]{2,1,0:T(8,128)(2,1)} %broadcast_in_dim.2), calls=%async_computation | async-start | bytes 2097152 | tf_op jit(solution)/shard_map/all_to_all | solution.py:15
  17.1 124.0 %copy-start.2 = (f32[1024]{0:T(1024)S(1)}, f32[1024]{0:T(1024)}, u32[]{:S(2)}) copy-start(f32[1024]{0:T(1024)} %param.9) | copy-start | bytes 12292
  17.1 124.0 %copy-start.3 = (f32[1024]{0:T(1024)S(1)}, f32[1024]{0:T(1024)}, u32[]{:S(2)}) copy-start(f32[1024]{0:T(1024)} %param.8) | copy-start | bytes 12292
  17.1 124.0 %copy-start.4 = (f32[512]{0:T(512)S(1)}, f32[512]{0:T(512)}, u32[]{:S(2)}) copy-start(f32[512]{0:T(512)} %param.11) | copy-start | bytes 6148
  17.1 346.6 %reduce-scatter.2.cloned.1.call-start = ((), (), s32[]{:S(2)}) async-start(), calls=%async_computation.4 | async-start | bytes 17825792 | tf_op jit(solution)/shard_map/reduce_scatter | solution.py:34
  89.2 3.4 copy-start
  159.1 204.6 %copy-start.1 = (f32[4096]{0:T(1024)S(1)}, f32[4096]{0:T(1024)}, u32[]{:S(2)}) copy-start(f32[4096]{0:T(1024)} %param.13) | copy-start | bytes 49156
Sparse Core Ops, SparseCore 0:
  9.8 79.4 all-gather.2
  91.0 50.1 all-gather.4
  159.3 204.3 reduce-scatter.1
where the time goes:
time: 373 us
  waiting for transfers between devices  325 us (87%)
  matrix products  18 us (5%)
  between operations  13.2 us (4%)
  starting transfers between devices  7.24 us (2%)
  other arithmetic  6.74 us (2%)
    reduce_scatter x1, waiting for transfers between devices, on_device(): lax.psum_scatter(jnp.dot(hidden, down_full, preferred_element_type=jnp.fl...  205 us
    all_gather x1, waiting for transfers between devices, on_device(): lax.all_gather(patch_tokens, 'tp', axis=0, tiled=True).astype(jnp.float32)  72.1 us
    all_gather x1, waiting for transfers between devices, on_device(): down_full = lax.all_gather(down_weight, 'img', axis=1, tiled=True)  47.1 us
    dot_general x1, matrix products, on_device(): jnp.dot(hidden, down_full, preferred_element_type=jnp.float32)  18 us
  transfers between devices with their start and end apart: 4, of which 3 were waited for; matrix products, arithmetic and copies ran while one was open for 2% of the time, Pallas kernels for 0%

commit v1 on v0

--- a/solution.py
+++ b/solution.py
@@ -30,7 +30,9 @@
         gathered, gather_directly(up_weight, "img", 0), preferred_element_type=jnp.float32
     )
     hidden = jax.nn.gelu(summed + up_bias).astype(jnp.bfloat16)
-    down_full = lax.all_gather(down_weight, "img", axis=1, tiled=True)
+    down_full = jnp.concatenate(
+        lax.all_to_all(jnp.stack([down_weight] * lax.axis_size("img")), "img", 0, 0), axis=1
+    )
     total = lax.psum_scatter(
         jnp.dot(hidden, down_full, preferred_element_type=jnp.float32).astype(jnp.bfloat16),
         "tp",

time: 373 us -> 359 us (0.962)
  waiting for transfers between devices: 325 us -> 302 us
  starting transfers between devices: 7.24 us -> 12.5 us
    all_gather x1 -> x0, waiting for transfers between devices: 47.1 us -> none  [on_device(): down_full = lax.all_gather(down_weight, 'img', axis=1, tiled=True)]
    all_to_all x1, waiting for transfers between devices: 0.01 us -> 13.8 us  [from_everyone(): return lax.all_to_all(copies, axis, split_axis=0, concat_axis=0, tiled=True)]
    all_to_all x0 -> x1, waiting for transfers between devices: none -> 6.47 us  [on_device(): lax.all_to_all(jnp.stack([down_weight] * lax.axis_size('img')), 'img', 0, 0)]
    all_to_all x0 -> x1, starting transfers between devices: none -> 5.25 us  [on_device(): lax.all_to_all(jnp.stack([down_weight] * lax.axis_size('img')), 'img', 0, 0)]
    all_gather x1, waiting for transfers between devices: 72.1 us -> 77.1 us  [on_device(): lax.all_gather(patch_tokens, 'tp', axis=0, tiled=True).astype(jnp.float32)]
  transfers between devices with their start and end apart: 4 -> 4, of which waited for: 3 -> 4; matrix products, arithmetic and copies ran while one was open for 2% -> 2% of each run, Pallas kernels for 0% -> 0%
where the time goes in v1:
time: 359 us; the launch traced here: 358 us
  waiting for transfers between devices  302 us (84%)
  matrix products  17.9 us (5%)
  between operations  13.5 us (4%)
  starting transfers between devices  12.5 us (3%)
  other arithmetic  6.74 us (2%)
  local copies, waits for them, and re-layouts  5.85 us (2%)
    reduce_scatter x1, waiting for transfers between devices, on_device(): lax.psum_scatter(jnp.dot(hidden, down_full, preferred_element_type=jnp.fl...  204 us
    all_gather x1, waiting for transfers between devices, on_device(): lax.all_gather(patch_tokens, 'tp', axis=0, tiled=True).astype(jnp.float32)  77.1 us
    dot_general x1, matrix products, on_device(): jnp.dot(hidden, down_full, preferred_element_type=jnp.float32)  17.9 us
    all_to_all x1, waiting for transfers between devices, from_everyone(): return lax.all_to_all(copies, axis, split_axis=0, concat_axis=0, tiled=True)  13.8 us
  transfers between devices with their start and end apart: 4, of which 4 were waited for; matrix products, arithmetic and copies ran while one was open for 2% of the time, Pallas kernels for 0%

profile of v1, /device:TPU:1, one launch (start us, length us, event | category | flops | bytes accessed | tf_op | source)
XLA Modules:
  0.0 358.5 jit_solution(2266810811509428176)
XLA Ops:
  6.5 1.9 broadcast_in_dim.2
  8.4 7.2 %all-to-all-start = ((bf16[16,64,512]{2,1,0:T(8,128)(2,1)}), bf16[16,64,512]{2,1,0:T(8,128)(2,1)S(1)}, u32[]{:S(2)}, u32[]{:S(2)}) async-start(bf16[16,64,512]{2,1,0:T(8,128)(2,1)} %broadcast_in_dim.2), calls=%async_computation | async-start | bytes 2097152 | tf_op jit(solution)/shard_map/all_to_all | solution.py:15
  15.6 0.0 all-gather.2.cloned.1.call-start
  15.6 0.7 all-gather.2.cloned.1.call-update
  16.3 1.1 copy.8
  17.4 13.8 %all-to-all-done = bf16[16,64,512]{2,1,0:T(8,128)(2,1)S(1)} async-done(((bf16[16,64,512]{2,1,0:T(8,128)(2,1)}), bf16[16,64,512]{2,1,0:T(8,128)(2,1)S(1)}, u32[]{:S(2)}, u32[]{:S(2)}) %all-to-all-start) | async-done | bytes 1048608 | tf_op jit(solution)/shard_map/all_to_all | solution.py:15
  31.3 2.4 stack.2
  33.6 5.2 %all-to-all-start.1 = ((bf16[16,512,256]{1,2,0:T(8,128)(2,1)}), bf16[16,512,256]{1,2,0:T(8,128)(2,1)}, u32[]{:S(2)}, u32[]{:S(2)}) async-start(bf16[16,512,256]{1,2,0:T(8,128)(2,1)} %stack.2), calls=%async_computation.1 | async-start | bytes 8388608 | tf_op jit(solution)/shard_map/all_to_all | solution.py:34
  38.9 0.0 copy-start.2
  38.9 0.0 copy-start.3
  38.9 0.0 copy-start.4
  38.9 0.0 reduce-scatter.2.cloned.1.call-start
  38.9 77.1 %all-gather.2.cloned.1.call-done = bf16[2048,1024]{1,0:T(8,128)(2,1)} async-done(((bf16[128,1024]{1,0:T(8,128)(2,1)}), bf16[2048,1024]{1,0:T(8,128)(2,1)}) %all-gather.2.cloned.1.call-update) | async-done | bytes 4194320 | tf_op jit(solution)/shard_map/all_gather | solution.py:23
  116.1 0.0 copy-start
  116.1 3.0 convert_reduce_fusion
  119.0 0.5 copy-done
  119.5 1.4 fusion.2
  120.9 6.5 %all-to-all-done.1 = bf16[16,512,256]{1,2,0:T(8,128)(2,1)} async-done(((bf16[16,512,256]{1,2,0:T(8,128)(2,1)}), bf16[16,512,256]{1,2,0:T(8,128)(2,1)}, u32[]{:S(2)}, u32[]{:S(2)}) %all-to-all-start.1) | async-done | bytes 4194336 | tf_op jit(solution)/shard_map/all_to_all | solution.py:34
  127.4 0.0 copy-done.2
  127.4 0.0 copy-done.3
  127.4 0.0 copy-done.4
  127.4 17.9 %convolution_convert_fusion = bf16[2048,4096]{1,0:T(8,128)(2,1)} fusion(bf16[512,4096]{0,1:T(8,128)(2,1)} %bitcast.2, bf16[1024,512]{1,0:T(8,128)(2,1)S(1)} %bitcast.6, bf16[2048,1024]{1,0:T(8,128)(2,1)} %all-gather.2.cloned.1.call-done, f32[1024]{0:T(1024)S(1)} %copy-done.2, f32[1024]{0:T(1024)S(1)} %copy-done.3, f32[2048]{0:T(1024)S(1)} %add_rsqrt_fusion, ...), kind=kOutput, calls=%fused_computation | convolution fusion | flops 10768875520 | bytes 26241024 | tf_op jit(solution)/shard_map/dot_general | solution.py:37
  145.3 0.0 copy-start.1
  145.3 0.0 reduce-scatter.2.cloned.1.call-update
  145.4 203.9 %reduce-scatter.2.cloned.1.call-done = bf16[128,4096]{1,0:T(8,128)(2,1)} async-done(((bf16[2048,4096]{1,0:T(8,128)(2,1)}), bf16[128,4096]{1,0:T(8,128)(2,1)}) %reduce-scatter.2.cloned.1.call-update) | async-done | bytes 1048592 | tf_op jit(solution)/shard_map/reduce_scatter | solution.py:36
  349.3 0.0 copy-done.1
  349.3 2.4 add_convert_fusion
  (2 shorter events, 0.0 us)
Async XLA Ops:
  8.4 22.8 %all-to-all-start = ((bf16[16,64,512]{2,1,0:T(8,128)(2,1)}), bf16[16,64,512]{2,1,0:T(8,128)(2,1)S(1)}, u32[]{:S(2)}, u32[]{:S(2)}) async-start(bf16[16,64,512]{2,1,0:T(8,128)(2,1)} %broadcast_in_dim.2), calls=%async_computation | async-start | bytes 2097152 | tf_op jit(solution)/shard_map/all_to_all | solution.py:15
  15.6 100.5 %all-gather.2.cloned.1.call-start = ((), (), s32[]{:S(2)}) async-start(), calls=%async_computation.3 | async-start | bytes 4456448 | tf_op jit(solution)/shard_map/all_gather | solution.py:23
  33.6 93.8 %all-to-all-start.1 = ((bf16[16,512,256]{1,2,0:T(8,128)(2,1)}), bf16[16,512,256]{1,2,0:T(8,128)(2,1)}, u32[]{:S(2)}, u32[]{:S(2)}) async-start(bf16[16,512,256]{1,2,0:T(8,128)(2,1)} %stack.2), calls=%async_computation.1 | async-start | bytes 8388608 | tf_op jit(solution)/shard_map/all_to_all | solution.py:34
  38.9 88.5 %copy-start.2 = (f32[1024]{0:T(1024)S(1)}, f32[1024]{0:T(1024)}, u32[]{:S(2)}) copy-start(f32[1024]{0:T(1024)} %param.9) | copy-start | bytes 12292
  38.9 88.5 %copy-start.3 = (f32[1024]{0:T(1024)S(1)}, f32[1024]{0:T(1024)}, u32[]{:S(2)}) copy-start(f32[1024]{0:T(1024)} %param.8) | copy-start | bytes 12292
  38.9 88.5 %copy-start.4 = (f32[512]{0:T(512)S(1)}, f32[512]{0:T(512)}, u32[]{:S(2)}) copy-start(f32[512]{0:T(512)} %param.11) | copy-start | bytes 6148
  38.9 310.4 %reduce-scatter.2.cloned.1.call-start = ((), (), s32[]{:S(2)}) async-start(), calls=%async_computation.4 | async-start | bytes 17825792 | tf_op jit(solution)/shard_map/reduce_scatter | solution.py:36
  116.1 3.4 copy-start
  145.3 203.9 %copy-start.1 = (f32[4096]{0:T(1024)S(1)}, f32[4096]{0:T(1024)}, u32[]{:S(2)}) copy-start(f32[4096]{0:T(1024)} %param.13) | copy-start | bytes 49156
Sparse Core Ops, SparseCore 0:
  18.8 97.1 all-gather.1
  145.5 203.7 reduce-scatter.1
